TPU v7x, 512 devices: a 8x2x16 block of a 8x8x16 slice. The times are simulated.
512 devices in a mesh: box: 2 (over y), gx: 128 (over z, x), gy: 2 (over core).
Axes of the slice: x: 8, y: 2, z: 16, core: 2. Of those that a mesh axis runs over, the one named last changes fastest.
The devices are a block of a 8x8x16 slice.
Arguments:
- positions: float32 [256, 4, 3, 256], P(('box', 'gx'), 'gy'), parts along dimension 0, may hold values from 0 to 18, as said below
- polarizability: float32 [256, 4, 256], P(('box', 'gx'), 'gy'), parts along dimension 0, may hold values from 0.3 to 1.5
- tile_counts: int32 [256, 4, 2], P(('box', 'gx'), 'gy'), parts along dimension 0, may hold values from 80 to 128, as said below
- molecules: int32 [256, 4, 256], P(('box', 'gx'), 'gy'), parts along dimension 0, may hold values from 0 to 170, as said below
- perm_field: float32 [256, 4, 3, 256], P(('box', 'gx'), 'gy'), parts along dimension 0, may hold values from -6 to 6
- dipoles: float32 [256, 4, 3, 256], P(('box', 'gx'), 'gy'), parts along dimension 0, may hold values from -4 to 4
- past_out: float32 [256, 4, 7, 3, 256], P(('box', 'gx'), 'gy'), parts along dimension 0, may hold values from -4 to 4
- past_res: float32 [256, 4, 7, 3, 256], P(('box', 'gx'), 'gy'), parts along dimension 0, may hold values from -15 to 15
Outputs:
- dipoles_next: float32 [256, 4, 3, 256], P(('box', 'gx'), 'gy'), parts along dimension 0
- diis_weights: float32 [16], P('box'), parts along dimension 0
There are 2 independent parts, one for each index of `box`. A program takes and returns all parts, laid end to end along the dimension named above; each array names one. Nothing has to cross between parts.
Inputs may be any that keep to these rules, and one draw needn't show every extreme that they name: x and y in [0, 9); z of an atom in z-tile t lies in [9 t, 9 t + 9); padded slots carry positions too. `tile_counts`: some z-tile is full. `molecules`: a group holds at most three atoms, all of one z-tile of one cell.
All inputs are finite; a program needn't handle non-finite values.
Results may differ from a plain program's by a relative error of at most 0.0003.
Values sent between devices are 32-bit elements; how exact they have to be, the bound alone decides.
No kernel may reach another device: no remote copies, remote signals or barrier semaphores. Data moves between devices by JAX's collectives and lax.ppermute only.
A program may use at most 64 MiB of HBM per device.

v0:
```python
import functools

import jax
import jax.numpy as jnp
from jax import lax
from jax.sharding import Mesh
from jax.sharding import PartitionSpec as P

ITERS = 2
GX = ("gx_0", "gx_1")
GX_GY = ("gx_0", "gx_1", "gy")
BOX_GX = ("box", "gx_0", "gx_1")


CELL_SIDE = 9.0
CUTOFF_SQ = 81.0
SOFTENING = 0.25
THOLE_DAMP = 0.39
FAR_LIFT = 1000.0
NEIGHBOUR_X = (1.0, 0.0, 1.0, 1.0)
NEIGHBOUR_Y = (0.0, 1.0, 1.0, -1.0)


def from_behind(block, axis, distance):
    devices = range(lax.axis_size(axis))
    route = [((i - distance) % len(devices), i) for i in devices]
    return lax.ppermute(block, axis, route)


def one_axis_at_a_time(array, axes):
    return functools.reduce(lax.psum, axes, array)


def pair_terms(
    target_coords,
    target_polar,
    target_groups,
    target_occupied,
    source_coords,
    source_polar,
    source_groups,
    source_occupied,
):
    displace = source_coords[:, None, :] - target_coords[:, :, None]
    square_dist = jnp.sum(displace * displace, axis=0) + SOFTENING
    distance = jnp.sqrt(square_dist)
    cube_dist = square_dist * distance
    damped = THOLE_DAMP * cube_dist / jnp.sqrt(target_polar[:, None] * source_polar[None, :])
    damping = jnp.exp(-damped)
    tapering = jnp.square(jnp.maximum(1.0 - square_dist / CUTOFF_SQ, 0.0))
    keeper = (target_groups[:, None] != source_groups[None, :]).astype(jnp.float32)
    weight = tapering * keeper * target_occupied[:, None] * source_occupied[None, :]
    isotropic = weight * -jnp.expm1(-damped) / cube_dist
    tensorial = 3.0 * weight * (1.0 - (1.0 + damped) * damping) / (cube_dist * square_dist)
    return (displace, isotropic, tensorial)


def field_targets(displace, isotropic, tensorial, source_dipole):
    projected = jnp.sum(displace * source_dipole[:, None, :], axis=0)
    return jnp.sum(displace * (tensorial * projected)[None], axis=2) - jnp.sum(
        isotropic[None] * source_dipole[:, None, :], axis=2
    )


def field_sources(displace, isotropic, tensorial, target_dipole):
    projected = jnp.sum(displace * target_dipole[:, :, None], axis=0)
    return jnp.sum(displace * (tensorial * projected)[None], axis=1) - jnp.sum(
        isotropic[None] * target_dipole[:, :, None], axis=1
    )


def tiled(values, filler, tile_count):
    shaped = values.reshape(values.shape[:-1] + (tile_count, values.shape[-1] // tile_count))
    widths = [(0, 0)] * (shaped.ndim - 2) + [(1, 1), (0, 0)]
    return jnp.pad(shaped, widths, constant_values=filler)


def padded_coords(coords, tile_count):
    marker = tiled(jnp.zeros_like(coords), 1.0, tile_count)
    lifted = jnp.array([0.0, 0.0, FAR_LIFT], jnp.float32).reshape(3, 1, 1)
    return tiled(coords, 0.0, tile_count) + marker * lifted


def band_sources(padded, tile_at):
    coords, polarity, groups, occupied, dipole = padded

    def flat_vector(member):
        window_part = lax.dynamic_slice_in_dim(member, tile_at, 3, 2)
        return jnp.transpose(window_part, (1, 0, 2, 3)).reshape(3, -1)

    def flat_scalar(member):
        return lax.dynamic_slice_in_dim(member, tile_at, 3, 1).reshape(-1)

    return (
        flat_vector(coords),
        flat_scalar(polarity),
        flat_scalar(groups),
        flat_scalar(occupied),
        flat_vector(dipole),
    )


def target_tile(own_cell, first_slot, tile_width):
    coords, polarity, groups, occupied = own_cell
    return (
        lax.dynamic_slice_in_dim(coords, first_slot, tile_width, 1),
        lax.dynamic_slice_in_dim(polarity, first_slot, tile_width, 0),
        lax.dynamic_slice_in_dim(groups, first_slot, tile_width, 0),
        lax.dynamic_slice_in_dim(occupied, first_slot, tile_width, 0),
    )


def four_static(packed):
    east_cells = from_behind(packed, GX, -1)
    next_own, next_east = from_behind((packed[0], east_cells[0]), "gy", -1)
    prior_east = from_behind(east_cells[-1], "gy", 1)
    north_cells = jnp.concatenate([packed[1:], next_own[None]], axis=0)
    north_east = jnp.concatenate([east_cells[1:], next_east[None]], axis=0)
    south_east = jnp.concatenate([prior_east[None], east_cells[:-1]], axis=0)
    return jnp.stack([east_cells, north_cells, north_east, south_east], axis=1)


def four_dipole(dipole):
    east_cells = from_behind(dipole, GX, -1)
    next_own, next_east = from_behind((dipole[0], east_cells[0]), "gy", -1)
    prior_east = from_behind(east_cells[-1], "gy", 1)
    north_cells = jnp.concatenate([dipole[1:], next_own[None]], axis=0)
    north_east = jnp.concatenate([east_cells[1:], next_east[None]], axis=0)
    south_east = jnp.concatenate([prior_east[None], east_cells[:-1]], axis=0)
    return jnp.stack([east_cells, north_cells, north_east, south_east], axis=1)


def half_statics(coords, polarity, groups, occupied, tile_count):
    cell_count = coords.shape[0]
    packed = jnp.concatenate([coords, polarity[:, None], occupied[:, None]], axis=1)
    nearby = four_static(packed)
    lift_x = jnp.array(NEIGHBOUR_X, jnp.float32) * CELL_SIDE
    lift_y = jnp.array(NEIGHBOUR_Y, jnp.float32) * CELL_SIDE
    lifted = jnp.stack([lift_x, lift_y, jnp.zeros_like(lift_x)], axis=1)
    nearby_coords = nearby[:, :, 0:3] + lifted[None, :, :, None]
    nearby_groups = jnp.full((cell_count, 4, coords.shape[-1]), -1, jnp.int32)
    own_padded = (
        padded_coords(coords[:, None], tile_count),
        tiled(polarity[:, None], 1.0, tile_count),
        tiled(groups[:, None], -1, tile_count),
        tiled(occupied[:, None], 0.0, tile_count),
    )
    nearby_padded = (
        padded_coords(nearby_coords, tile_count),
        tiled(nearby[:, :, 3], 1.0, tile_count),
        tiled(nearby_groups, -1, tile_count),
        tiled(nearby[:, :, 4], 0.0, tile_count),
    )
    return (own_padded, nearby_padded)


def half_cell(own_cell, own_band, nearby_band, dipole, tile_count):
    tile_width = dipole.shape[-1] // tile_count

    def one_tile(tile_at, carry):
        own_field, back_field = carry
        first_slot = tile_at * tile_width
        target = target_tile(own_cell, first_slot, tile_width)
        target_dipole = lax.dynamic_slice_in_dim(dipole, first_slot, tile_width, 1)
        source = band_sources(own_band, tile_at)
        displace, isotropic, tensorial = pair_terms(
            target[0], target[1], target[2], target[3], source[0], source[1], source[2], source[3]
        )
        inside = field_targets(displace, isotropic, tensorial, source[4])
        source = band_sources(nearby_band, tile_at)
        displace, isotropic, tensorial = pair_terms(
            target[0], target[1], target[2], target[3], source[0], source[1], source[2], source[3]
        )
        outside = field_targets(displace, isotropic, tensorial, source[4])
        returned = field_sources(displace, isotropic, tensorial, target_dipole)
        returned = jnp.transpose(returned.reshape(3, 4, 3, tile_width), (1, 0, 2, 3))
        own_field = lax.dynamic_update_slice_in_dim(own_field, inside + outside, first_slot, 1)
        window = lax.dynamic_slice_in_dim(back_field, tile_at, 3, 2) + returned
        back_field = lax.dynamic_update_slice_in_dim(back_field, window, tile_at, 2)
        return (own_field, back_field)

    initial = (
        jnp.zeros(dipole.shape, jnp.float32),
        jnp.zeros((4, 3, tile_count + 2, tile_width), jnp.float32),
    )
    own_field, back_field = lax.fori_loop(0, tile_count, one_tile, initial)
    return (own_field, back_field[:, :, 1:-1].reshape(4, 3, -1))


def half_field(own_cells, statics, dipole, tile_count):
    own_padded, nearby_padded = statics
    own_band = own_padded + (tiled(dipole[:, None], 0.0, tile_count),)
    nearby_band = nearby_padded + (tiled(four_dipole(dipole), 0.0, tile_count),)

    def per_cell(members):
        return half_cell(members[0], members[1], members[2], members[3], tile_count)

    own_field, back_field = lax.map(per_cell, (own_cells, own_band, nearby_band, dipole))
    north_part = back_field[:, 1]
    north_east = back_field[:, 2]
    south_east = back_field[:, 3]
    from_below, below_east = from_behind((north_part[-1], north_east[-1]), "gy", 1)
    from_above = from_behind(south_east[0], "gy", -1)
    from_south = jnp.concatenate([from_below[None], north_part[:-1]], axis=0)
    from_south_west = jnp.concatenate([below_east[None], north_east[:-1]], axis=0)
    from_north = jnp.concatenate([south_east[1:], from_above[None]], axis=0)
    eastward = back_field[:, 0] + from_south_west + from_north
    from_west = from_behind(eastward, GX, 1)
    return own_field + from_south + from_west


def diis_weights(gram_matrix):
    lower = jnp.linalg.cholesky(gram_matrix)
    history = gram_matrix.shape[0]
    forward = []
    for row_at in range(history):
        running = jnp.ones((), gram_matrix.dtype)
        for col_at in range(row_at):
            running = running - lower[row_at, col_at] * forward[col_at]
        forward.append(running / lower[row_at, row_at])
    backward = [None] * history
    for row_at in reversed(range(history)):
        running = forward[row_at]
        for col_at in range(row_at + 1, history):
            running = running - lower[col_at, row_at] * backward[col_at]
        backward[row_at] = running / lower[row_at, row_at]
    solved = jnp.stack(backward)
    return solved / jnp.sum(solved)


def body(
    positions, polarizability, tile_counts, molecules, perm_field, dipoles, past_out, past_res
):
    counts = tile_counts[0]
    cell_count = counts.shape[0]
    tile_count = counts.shape[1]
    coords = positions[0]
    atom_slots = coords.shape[-1]
    tile_width = atom_slots // tile_count
    slot_index = lax.broadcasted_iota(jnp.int32, (cell_count, tile_count, tile_width), 2)
    occupied = (slot_index < counts[:, :, None]).astype(jnp.float32).reshape(cell_count, atom_slots)
    polarity = polarizability[0]
    groups = molecules[0]
    own_cells = (coords, polarity, groups, occupied)
    occupied_vec = occupied[:, None, :]
    scaled = occupied_vec * polarity[:, None, :]
    stored_out = jnp.moveaxis(past_out[0], 1, 0) * occupied_vec
    stored_res = jnp.moveaxis(past_res[0], 1, 0) * occupied_vec
    current = dipoles[0] * occupied_vec
    permanent = perm_field[0]
    statics = half_statics(coords, polarity, groups, occupied, tile_count)
    weights = jnp.zeros((stored_out.shape[0] + 1,), jnp.float32)
    for step_at in range(ITERS):
        induced = half_field(own_cells, statics, current, tile_count)
        jacobi = scaled * (permanent + induced)
        residual = jacobi - current
        outputs_all = jnp.concatenate([stored_out, jacobi[None]], 0)
        residual_all = jnp.concatenate([stored_res, residual[None]], 0)
        flattened = residual_all.reshape(residual_all.shape[0], -1)
        local_gram = jnp.dot(
            flattened,
            flattened.T,
            precision=lax.Precision.HIGHEST,
            preferred_element_type=jnp.float32,
        )
        gram_matrix = one_axis_at_a_time(local_gram, GX_GY)
        weights = diis_weights(gram_matrix)
        current = jnp.sum(weights[:, None, None, None] * outputs_all, axis=0)
        stored_out = outputs_all[1:]
        stored_res = residual_all[1:]
    return (current[None], weights)


def solution(mesh):
    torus = Mesh(
        mesh.devices.reshape(mesh.shape["box"], 16, 8, mesh.shape["gy"]),
        ("box", "gx_0", "gx_1", "gy"),
    )
    return jax.shard_map(
        body,
        mesh=torus,
        in_specs=(
            P(BOX_GX, "gy", None, None),
            P(BOX_GX, "gy", None),
            P(BOX_GX, "gy", None),
            P(BOX_GX, "gy", None),
            P(BOX_GX, "gy", None, None),
            P(BOX_GX, "gy", None, None),
            P(BOX_GX, "gy", None, None, None),
            P(BOX_GX, "gy", None, None, None),
        ),
        out_specs=(P(BOX_GX, "gy", None, None), P("box")),
        check_vma=False,
    )
```

profile of v0, /device:TPU:80, one launch (start us, length us, event | category | flops | bytes accessed | tf_op | source)
XLA Modules:
  0.0 355.8 jit_solution(4222490422173814434)
XLA Ops:
  2.1 47.3 %collective-permute-start.4 = (f32[2,3,256]{2,1,0:T(4,128)S(1)}, f32[2,3,256]{2,1,0:T(4,128)S(1)}, u32[]{:S(2)}, u32[]{:S(2)}) collective-permute-start(f32[2,3,256]{2,1,0:T(4,128)S(1)} %bitcast_multiply_fusion.2), channel_id=1, source_target_pairs={{2,0},{4,2},{6,4},{8,6},{10,8},{12,10},{14,12},{16,14},{18,16},{20... | collective-permute-start | bytes 18440 | tf_op jit(solution)/shard_map/ppermute | solution.py:27
  53.5 3.2 collective-permute-start
  56.8 2.2 collective-permute-start.1
  64.2 2.2 collective-permute-start.7
  66.5 2.2 collective-permute-start.6
  69.6 2.2 collective-permute-start.3
  71.8 2.2 collective-permute-start.2
  75.4 23.1 %while.55 = (s32[]{:T(128)}, f32[2,3,256]{2,1,0:T(4,128)S(1)}, f32[2,4,3,256]{3,1,2,0:T(4,128)S(1)}, f32[2,3,256]{2,1,0:T(4,128)S(1)}, f32[2,256]{1,0:T(2,128)S(...) while((s32[]{:T(128)}, f32[2,3,256]{2,1,0:T(4,128)S(1)}, ...), condition=%wide.region_14.15_spmd, body=%wide.region_0.14_spmd.sunk | while | flops 19906180 | bytes 14344956 | solution.py:198
  75.6 11.3 %while.58 = (s32[]{:T(128)}, f32[3,256]{1,0:T(4,128)S(1)}, f32[4,3,4,128]{3,2,0,1:T(4,128)S(1)}, f32[1,3,4,128]{3,2,1,0:T(4,128)S(1)}, f32[3,256]{1,0:T(4,128)S(...) while((s32[]{:T(128)}, f32[3,256]{1,0:T(4,128)S(1)}, ...), condition=%wide.region_13.13_spmd, body=%wide.region_1.12_spmd.sunk | while | flops 19906180 | bytes 14031151 | solution.py:186
  87.1 11.3 %while.58 = (s32[]{:T(128)}, f32[3,256]{1,0:T(4,128)S(1)}, f32[4,3,4,128]{3,2,0,1:T(4,128)S(1)}, f32[1,3,4,128]{3,2,1,0:T(4,128)S(1)}, f32[3,256]{1,0:T(4,128)S(...) while((s32[]{:T(128)}, f32[3,256]{1,0:T(4,128)S(1)}, ...), condition=%wide.region_13.13_spmd, body=%wide.region_1.12_spmd.sunk | while | flops 19906180 | bytes 14031151 | solution.py:186
  98.5 2.2 collective-permute-start.10
  100.8 2.2 collective-permute-start.9
  103.0 2.2 collective-permute-start.8
  105.3 2.7 collective-permute-start.11
  108.0 6.2 %collective-permute-done.11 = f32[2,3,256]{2,1,0:T(4,128)S(1)} collective-permute-done((f32[2,3,256]{2,1,0:T(4,128)S(1)}, f32[2,3,256]{2,1,0:T(4,128)S(1)}, u32[]{:S(2)}, u32[]{:S(2)}) %collective-permute-start.11) | collective-permute-done | bytes 6176 | tf_op jit(solution)/shard_map/ppermute | solution.py:27
  114.4 27.1 %psum.42 = f32[8,8]{0,1:T(8,128)S(1)} all-reduce(f32[8,8]{0,1:T(8,128)S(1)} %convolution_bitcast_fusion.1), channel_id=1, replica_groups=mesh['box'=2,'gx_0'=16,'gx_1'=8,'gy'=2] {'gx_0'}, use_global_device_ids=true, to_apply=%region_15.16 | all-reduce | flops 64 | bytes 512 | tf_op jit(solution)/shard_map/psum | solution.py:31
  141.5 14.4 %psum.43 = f32[8,8]{0,1:T(8,128)S(1)} all-reduce(f32[8,8]{0,1:T(8,128)S(1)} %psum.42), channel_id=1, replica_groups=mesh['box'=2,'gx_0'=16,'gx_1'=8,'gy'=2] {'gx_1'}, use_global_device_ids=true, to_apply=%region_16.17 | all-reduce | flops 64 | bytes 512 | tf_op jit(solution)/shard_map/psum | solution.py:31
  155.9 2.5 psum.44
  208.1 5.1 %collective-permute-start.12 = (f32[2,3,256]{2,1,0:T(4,128)S(1)}, f32[2,3,256]{2,1,0:T(4,128)S(1)}, u32[]{:S(2)}, u32[]{:S(2)}) collective-permute-start(f32[2,3,256]{2,1,0:T(4,128)S(1)} %fusion.59), channel_id=1, source_target_pairs={{2,0},{4,2},{6,4},{8,6},{10,8},{12,10},{14,12},{16,14},{18,16},{20... | collective-permute-start | bytes 18440 | tf_op jit(solution)/shard_map/ppermute | solution.py:27
  215.2 2.4 collective-permute-start.15
  217.7 2.1 collective-permute-start.14
  220.8 23.1 %while.57 = (s32[]{:T(128)}, f32[2,3,256]{2,1,0:T(4,128)S(1)}, f32[2,4,3,256]{3,1,2,0:T(4,128)S(1)}, f32[2,3,256]{2,1,0:T(4,128)S(1)}, f32[2,256]{1,0:T(2,128)S(...) while((s32[]{:T(128)}, f32[2,3,256]{2,1,0:T(4,128)S(1)}, ...), condition=%wide.region_35.37_spmd, body=%wide.region_21.36_spmd.sunk | while | flops 19906180 | bytes 14344960 | solution.py:198
  221.1 11.3 %while.59 = (s32[]{:T(128)}, f32[3,256]{1,0:T(4,128)S(1)}, f32[4,3,4,128]{3,2,0,1:T(4,128)S(1)}, f32[1,3,4,128]{3,2,1,0:T(4,128)S(1)}, f32[3,256]{1,0:T(4,128)S(...) while((s32[]{:T(128)}, f32[3,256]{1,0:T(4,128)S(1)}, ...), condition=%wide.region_34.35_spmd, body=%wide.region_22.34_spmd.sunk | while | flops 19906180 | bytes 14031151 | solution.py:186
  232.6 11.3 %while.59 = (s32[]{:T(128)}, f32[3,256]{1,0:T(4,128)S(1)}, f32[4,3,4,128]{3,2,0,1:T(4,128)S(1)}, f32[1,3,4,128]{3,2,1,0:T(4,128)S(1)}, f32[3,256]{1,0:T(4,128)S(...) while((s32[]{:T(128)}, f32[3,256]{1,0:T(4,128)S(1)}, ...), condition=%wide.region_34.35_spmd, body=%wide.region_22.34_spmd.sunk | while | flops 19906180 | bytes 14031151 | solution.py:186
  244.0 2.1 collective-permute-start.18
  246.1 2.3 collective-permute-start.17
  248.5 2.1 collective-permute-start.16
  250.6 2.0 collective-permute-start.19
  252.7 6.9 %collective-permute-done.19 = f32[2,3,256]{2,1,0:T(4,128)S(1)} collective-permute-done((f32[2,3,256]{2,1,0:T(4,128)S(1)}, f32[2,3,256]{2,1,0:T(4,128)S(1)}, u32[]{:S(2)}, u32[]{:S(2)}) %collective-permute-start.19) | collective-permute-done | bytes 6176 | tf_op jit(solution)/shard_map/ppermute | solution.py:27
  259.7 27.1 %psum.45 = f32[8,8]{0,1:T(8,128)S(1)} all-reduce(f32[8,8]{0,1:T(8,128)S(1)} %convolution_bitcast_fusion), channel_id=1, replica_groups=mesh['box'=2,'gx_0'=16,'gx_1'=8,'gy'=2] {'gx_0'}, use_global_device_ids=true, to_apply=%region_36.38 | all-reduce | flops 64 | bytes 512 | tf_op jit(solution)/shard_map/psum | solution.py:31
  286.9 16.2 %psum.46 = f32[8,8]{0,1:T(8,128)S(1)} all-reduce(f32[8,8]{0,1:T(8,128)S(1)} %psum.45), channel_id=1, replica_groups=mesh['box'=2,'gx_0'=16,'gx_1'=8,'gy'=2] {'gx_1'}, use_global_device_ids=true, to_apply=%region_37.39 | all-reduce | flops 64 | bytes 512 | tf_op jit(solution)/shard_map/psum | solution.py:31
  303.0 2.5 psum.47
  (468 shorter events, 69.1 us)
Async XLA Ops:
  0.6 74.5 %copy-start.6 = (f32[3]{0:T(128)S(1)}, f32[3]{0:T(128)}, u32[]{:S(2)}) copy-start(f32[3]{0:T(128)} %constant.290.clone) | copy-start | bytes 40
  0.6 74.3 %copy-start.7 = (f32[4,3]{1,0:T(4,128)S(1)}, f32[4,3]{1,0:T(4,128)}, u32[]{:S(2)}) copy-start(f32[4,3]{1,0:T(4,128)} %constant.329) | copy-start | bytes 148
  0.7 74.7 %copy-start = (f32[1,2,256]{2,1,0:T(2,128)S(1)}, f32[1,2,256]{2,1,0:T(2,128)}, u32[]{:S(2)}) copy-start(f32[1,2,256]{2,1,0:T(2,128)} %param.22) | copy-start | bytes 6148
  0.7 74.6 %copy-start.1 = (s32[1,2,256]{2,1,0:T(2,128)S(1)}, s32[1,2,256]{2,1,0:T(2,128)}, u32[]{:S(2)}) copy-start(s32[1,2,256]{2,1,0:T(2,128)} %param.24) | copy-start | bytes 6148
  2.1 62.1 %collective-permute-start.4 = (f32[2,3,256]{2,1,0:T(4,128)S(1)}, f32[2,3,256]{2,1,0:T(4,128)S(1)}, u32[]{:S(2)}, u32[]{:S(2)}) collective-permute-start(f32[2,3,256]{2,1,0:T(4,128)S(1)} %bitcast_multiply_fusion.2), channel_id=1, source_target_pairs={{2,0},{4,2},{6,4},{8,6},{10,8},{12,10},{14,12},{16,14},{18,16},{20... | collective-permute-start | bytes 18440 | tf_op jit(solution)/shard_map/ppermute | solution.py:27
  49.4 14.8 %collective-permute-start.5 = (f32[3,256]{1,0:T(4,128)S(1)}, f32[3,256]{1,0:T(4,128)S(1)}, u32[]{:S(2)}, u32[]{:S(2)}) collective-permute-start(f32[3,256]{1,0:T(4,128)S(1)} %get-tuple-element.1237), channel_id=1, source_target_pairs={{1,0},{0,1},{3,2},{2,3},{5,4},{4,5},{7,6},{6,7},{9,8},{8,9},{11,10... | collective-permute-start | bytes 9224 | tf_op jit(solution)/shard_map/ppermute | solution.py:27
  53.5 16.0 %collective-permute-start = (f32[2,5,256]{2,1,0:T(8,128)S(1)}, f32[2,5,256]{2,1,0:T(8,128)S(1)}, u32[]{:S(2)}, u32[]{:S(2)}) collective-permute-start(f32[2,5,256]{2,1,0:T(8,128)S(1)} %pad_maximum_fusion.4), channel_id=1, source_target_pairs={{2,0},{4,2},{6,4},{8,6},{10,8},{12,10},{14,12},{16,14},{18,16},{20... | collective-permute-start | bytes 30728 | tf_op jit(solution)/shard_map/ppermute | solution.py:27
  56.8 11.8 %collective-permute-start.1 = (f32[5,256]{1,0:T(8,128)S(1)}, f32[5,256]{1,0:T(8,128)S(1)}, u32[]{:S(2)}, u32[]{:S(2)}) collective-permute-start(f32[5,256]{1,0:T(8,128)S(1)} %get-tuple-element.1225), channel_id=1, source_target_pairs={{1,0},{0,1},{3,2},{2,3},{5,4},{4,5},{7,6},{6,7},{9,8},{8,9},{11,10... | collective-permute-start | bytes 15368 | tf_op jit(solution)/shard_map/ppermute | solution.py:27
  64.2 4.5 %collective-permute-start.7 = (f32[3,256]{1,0:T(4,128)S(1)}, f32[3,256]{1,0:T(4,128)S(1)}, u32[]{:S(2)}, u32[]{:S(2)}) collective-permute-start(f32[3,256]{1,0:T(4,128)S(1)} %get-tuple-element.1239), channel_id=1, source_target_pairs={{1,0},{0,1},{3,2},{2,3},{5,4},{4,5},{7,6},{6,7},{9,8},{8,9},{11,10... | collective-permute-start | bytes 9224 | tf_op jit(solution)/shard_map/ppermute | solution.py:27
  66.5 3.1 collective-permute-start.6
  69.6 4.4 %collective-permute-start.3 = (f32[5,256]{1,0:T(8,128)S(1)}, f32[5,256]{1,0:T(8,128)S(1)}, u32[]{:S(2)}, u32[]{:S(2)}) collective-permute-start(f32[5,256]{1,0:T(8,128)S(1)} %get-tuple-element.1227), channel_id=1, source_target_pairs={{1,0},{0,1},{3,2},{2,3},{5,4},{4,5},{7,6},{6,7},{9,8},{8,9},{11,10... | collective-permute-start | bytes 15368 | tf_op jit(solution)/shard_map/ppermute | solution.py:27
  71.8 3.1 collective-permute-start.2
  75.3 27.6 %copy-start.3 = (f32[1,2,7,3,256]{4,1,3,2,0:T(2,128)S(1)}, f32[1,2,7,3,256]{4,1,3,2,0:T(2,128)}, u32[]{:S(2)}) copy-start(f32[1,2,7,3,256]{4,1,3,2,0:T(2,128)} %param.28) | copy-start | bytes 129028
  75.3 27.6 %copy-start.4 = (f32[1,2,7,3,256]{4,1,3,2,0:T(2,128)S(1)}, f32[1,2,7,3,256]{4,1,3,2,0:T(2,128)}, u32[]{:S(2)}) copy-start(f32[1,2,7,3,256]{4,1,3,2,0:T(2,128)} %param.27) | copy-start | bytes 129028
  75.3 38.8 %copy-start.2 = (f32[1,2,3,256]{3,1,2,0:T(2,128)S(1)}, f32[1,2,3,256]{3,1,2,0:T(2,128)}, u32[]{:S(2)}) copy-start(f32[1,2,3,256]{3,1,2,0:T(2,128)} %param.26) | copy-start | bytes 18436
  75.4 38.8 %copy-start.5 = (f32[1,2,3,256]{3,1,2,0:T(2,128)S(1)}, f32[1,2,3,256]{3,1,2,0:T(2,128)}, u32[]{:S(2)}) copy-start(f32[1,2,3,256]{3,1,2,0:T(2,128)} %param.25) | copy-start | bytes 18436
  98.5 6.7 %collective-permute-start.10 = (f32[3,256]{1,0:T(4,128)S(1)}, f32[3,256]{1,0:T(4,128)S(1)}, u32[]{:S(2)}, u32[]{:S(2)}) collective-permute-start(f32[3,256]{1,0:T(4,128)S(1)} %get-tuple-element.1219), channel_id=1, source_target_pairs={{1,0},{0,1},{3,2},{2,3},{5,4},{4,5},{7,6},{6,7},{9,8},{8,9},{11,10... | collective-permute-start | bytes 9224 | tf_op jit(solution)/shard_map/ppermute | solution.py:27
  100.8 4.5 %collective-permute-start.9 = (f32[3,256]{1,0:T(4,128)S(1)}, f32[3,256]{1,0:T(4,128)S(1)}, u32[]{:S(2)}, u32[]{:S(2)}) collective-permute-start(f32[3,256]{1,0:T(4,128)S(1)} %get-tuple-element.1222), channel_id=1, source_target_pairs={{1,0},{0,1},{3,2},{2,3},{5,4},{4,5},{7,6},{6,7},{9,8},{8,9},{11,10... | collective-permute-start | bytes 9224 | tf_op jit(solution)/shard_map/ppermute | solution.py:27
  103.0 5.0 %collective-permute-start.8 = (f32[3,256]{1,0:T(4,128)S(1)}, f32[3,256]{1,0:T(4,128)S(1)}, u32[]{:S(2)}, u32[]{:S(2)}) collective-permute-start(f32[3,256]{1,0:T(4,128)S(1)} %get-tuple-element.1218), channel_id=1, source_target_pairs={{1,0},{0,1},{3,2},{2,3},{5,4},{4,5},{7,6},{6,7},{9,8},{8,9},{11,10... | collective-permute-start | bytes 9224 | tf_op jit(solution)/shard_map/ppermute | solution.py:27
  105.3 8.9 %collective-permute-start.11 = (f32[2,3,256]{2,1,0:T(4,128)S(1)}, f32[2,3,256]{2,1,0:T(4,128)S(1)}, u32[]{:S(2)}, u32[]{:S(2)}) collective-permute-start(f32[2,3,256]{2,1,0:T(4,128)S(1)} %fusion.77), channel_id=1, source_target_pairs={{254,0},{0,2},{2,4},{4,6},{6,8},{8,10},{10,12},{12,14},{14,16},{16... | collective-permute-start | bytes 18440 | tf_op jit(solution)/shard_map/ppermute | solution.py:27
  208.1 7.1 %collective-permute-start.12 = (f32[2,3,256]{2,1,0:T(4,128)S(1)}, f32[2,3,256]{2,1,0:T(4,128)S(1)}, u32[]{:S(2)}, u32[]{:S(2)}) collective-permute-start(f32[2,3,256]{2,1,0:T(4,128)S(1)} %fusion.59), channel_id=1, source_target_pairs={{2,0},{4,2},{6,4},{8,6},{10,8},{12,10},{14,12},{16,14},{18,16},{20... | collective-permute-start | bytes 18440 | tf_op jit(solution)/shard_map/ppermute | solution.py:27
  213.2 6.6 %collective-permute-start.13 = (f32[3,256]{1,0:T(4,128)S(1)}, f32[3,256]{1,0:T(4,128)S(1)}, u32[]{:S(2)}, u32[]{:S(2)}) collective-permute-start(f32[3,256]{1,0:T(4,128)S(1)} %get-tuple-element.1231), channel_id=1, source_target_pairs={{1,0},{0,1},{3,2},{2,3},{5,4},{4,5},{7,6},{6,7},{9,8},{8,9},{11,10... | collective-permute-start | bytes 9224 | tf_op jit(solution)/shard_map/ppermute | solution.py:27
  215.2 4.7 %collective-permute-start.15 = (f32[3,256]{1,0:T(4,128)S(1)}, f32[3,256]{1,0:T(4,128)S(1)}, u32[]{:S(2)}, u32[]{:S(2)}) collective-permute-start(f32[3,256]{1,0:T(4,128)S(1)} %get-tuple-element.1233), channel_id=1, source_target_pairs={{1,0},{0,1},{3,2},{2,3},{5,4},{4,5},{7,6},{6,7},{9,8},{8,9},{11,10... | collective-permute-start | bytes 9224 | tf_op jit(solution)/shard_map/ppermute | solution.py:27
  217.7 3.1 collective-permute-start.14
  244.0 6.6 %collective-permute-start.18 = (f32[3,256]{1,0:T(4,128)S(1)}, f32[3,256]{1,0:T(4,128)S(1)}, u32[]{:S(2)}, u32[]{:S(2)}) collective-permute-start(f32[3,256]{1,0:T(4,128)S(1)} %bitcast.454), channel_id=1, source_target_pairs={{1,0},{0,1},{3,2},{2,3},{5,4},{4,5},{7,6},{6,7},{9,8},{8,9},{11,10... | collective-permute-start | bytes 9224 | tf_op jit(solution)/shard_map/ppermute | solution.py:27
  246.1 4.5 %collective-permute-start.17 = (f32[3,256]{1,0:T(4,128)S(1)}, f32[3,256]{1,0:T(4,128)S(1)}, u32[]{:S(2)}, u32[]{:S(2)}) collective-permute-start(f32[3,256]{1,0:T(4,128)S(1)} %get-tuple-element.1216), channel_id=1, source_target_pairs={{1,0},{0,1},{3,2},{2,3},{5,4},{4,5},{7,6},{6,7},{9,8},{8,9},{11,10... | collective-permute-start | bytes 9224 | tf_op jit(solution)/shard_map/ppermute | solution.py:27
  248.5 4.2 %collective-permute-start.16 = (f32[3,256]{1,0:T(4,128)S(1)}, f32[3,256]{1,0:T(4,128)S(1)}, u32[]{:S(2)}, u32[]{:S(2)}) collective-permute-start(f32[3,256]{1,0:T(4,128)S(1)} %get-tuple-element.1213), channel_id=1, source_target_pairs={{1,0},{0,1},{3,2},{2,3},{5,4},{4,5},{7,6},{6,7},{9,8},{8,9},{11,10... | collective-permute-start | bytes 9224 | tf_op jit(solution)/shard_map/ppermute | solution.py:27
  250.6 8.9 %collective-permute-start.19 = (f32[2,3,256]{2,1,0:T(4,128)S(1)}, f32[2,3,256]{2,1,0:T(4,128)S(1)}, u32[]{:S(2)}, u32[]{:S(2)}) collective-permute-start(f32[2,3,256]{2,1,0:T(4,128)S(1)} %fusion.75), channel_id=1, source_target_pairs={{254,0},{0,2},{2,4},{4,6},{6,8},{8,10},{10,12},{12,14},{14,16},{16... | collective-permute-start | bytes 18440 | tf_op jit(solution)/shard_map/ppermute | solution.py:27
  355.1 0.7 copy-start.8
where the time goes:
time: 359 us; the launch traced here: 356 us
  between operations  93.1 us (26%)
  starting transfers between devices  92.8 us (26%)
  blocking collectives  89.9 us (25%)
  other arithmetic  47 us (13%)
  waiting for transfers between devices  15.6 us (4%)
  local copies, waits for them, and re-layouts  15.3 us (4%)
    ppermute x20, starting transfers between devices, from_behind(): return lax.ppermute(block, axis, route)  92.8 us
    psum x6, blocking collectives, one_axis_at_a_time(): return functools.reduce(lax.psum, axes, array)  89.9 us
    ppermute x20, waiting for transfers between devices, from_behind(): return lax.ppermute(block, axis, route)  15.6 us
    div x16, other arithmetic, pair_terms(): isotropic = weight * -jnp.expm1(-damped) / cube_dist  10.8 us
    reduce_sum x8, other arithmetic, field_sources(): projected = jnp.sum(displace * target_dipole[:, :, None], axis=0)  8.01 us
    mul x8, other arithmetic, field_targets(): tensorial * projected  7.77 us
  transfers between devices with their start and end apart: 20, of which 5 were waited for; matrix products, arithmetic and copies ran while one was open for 2% of the time, Pallas kernels for 0%

commit v1 on v0

v1 whole, which is shorter than its diff:
```python
import functools

import jax
import jax.numpy as jnp
from jax import lax
from jax.experimental import pallas as pl
from jax.experimental.pallas import tpu as pltpu
from jax.sharding import Mesh
from jax.sharding import PartitionSpec as P

GX = ("gx_0", "gx_1")
BOX_GX = ("box", "gx_0", "gx_1")
TORUS_Z = 16
TORUS_X = 8

CELL_SIDE = 9.0
CUTOFF_SQ = 81.0
SOFTENING = 0.25
THOLE_DAMP = 0.39
LN2 = 0.6931471805599453

NVEC = 8
ROW_XYZ = 24
ROW_POLAR = 27
ROW_OCC = 28
ROW_PERM = 29
ROWS = 32
COMPS = 16
BLOCKS = 18
CHUNK = 16
F32 = jnp.float32
BF16 = jnp.bfloat16


def vmem():
    return pl.BlockSpec(memory_space=pltpu.VMEM)


def smem():
    return pl.BlockSpec(memory_space=pltpu.SMEM)


def split3(value):
    first = value.astype(BF16)
    rest = value - first.astype(F32)
    second = rest.astype(BF16)
    third = (rest - second.astype(F32)).astype(BF16)
    return first, second, third


def split2(value):
    first = value.astype(BF16)
    return first, (value - first.astype(F32)).astype(BF16)


def pack_kernel(counts, positions, polarity, permanent, dipoles, past_out, packed):
    cells = positions.shape[0]
    slots = positions.shape[-1]
    tile = slots // counts.shape[1]
    slot = lax.broadcasted_iota(jnp.int32, (1, slots), 1)
    for cell in range(cells):
        occ = (slot < counts[cell, 0]).astype(F32)
        for t in range(1, counts.shape[1]):
            inside = (slot - t * tile < counts[cell, t]).astype(F32)
            occ = jnp.where(slot >= t * tile, inside, occ)
        for comp in range(3):
            for k in range(NVEC - 1):
                row = past_out[cell, k, comp : comp + 1, :] * occ
                packed[cell, comp * NVEC + k : comp * NVEC + k + 1, :] = row
            row = dipoles[cell, comp : comp + 1, :] * occ
            packed[cell, comp * NVEC + NVEC - 1 : comp * NVEC + NVEC, :] = row
            centre = 0.5 * CELL_SIDE if comp < 2 else CELL_SIDE
            row = positions[cell, comp : comp + 1, :] - centre
            packed[cell, ROW_XYZ + comp : ROW_XYZ + comp + 1, :] = row
            row = permanent[cell, comp : comp + 1, :]
            packed[cell, ROW_PERM + comp : ROW_PERM + comp + 1, :] = row
        packed[cell, ROW_POLAR : ROW_POLAR + 1, :] = polarity[cell : cell + 1, :]
        packed[cell, ROW_OCC : ROW_OCC + 1, :] = occ


def source_moments(coords, vectors):
    vx, vy, vz = vectors
    dot = coords[0] * vx + coords[1] * vy + coords[2] * vz
    comps = [coords[i] * dot for i in range(3)]
    comps += [coords[i] * vectors[j] for i in range(3) for j in range(3)]
    return comps + [dot, vx, vy, vz]


def fields_of(moments, isotropic, target):
    along = target[0] * moments[13] + target[1] * moments[14] + target[2] * moments[15]
    shared = moments[12] - along
    out = []
    for i in range(3):
        part = moments[i] - target[i] * shared
        for j in range(3):
            part = part - target[j] * moments[3 + 3 * i + j]
        out.append(3.0 * part - isotropic[i])
    return out


def block_of(index, core, cells):
    near = index < 12
    own_at = jnp.maximum(index - 12, 0)
    step = lax.rem(index, 3) - 1
    own_target = 2 * core + own_at // 3
    target = jnp.where(near, lax.rem(index // 3 - step + cells, cells), own_target)
    source = jnp.where(
        near, index // 3, cells + lax.rem(own_target + step + cells, cells)
    )
    side = jnp.where(near, 1 - 2 * core, 0)
    move_x = side.astype(F32) * CELL_SIDE
    move_y = step.astype(F32) * CELL_SIDE
    inside = jnp.logical_and(index >= 12, step == 0)
    return source, target, own_at // 3, inside, move_x, move_y


def moved_target(rows, move_x, move_y):
    return (rows[0:1] - move_x, rows[1:2] - move_y, rows[2:3])


def pair_kernel(column, beside, groups, fields, pairs, moments, sources):
    cells = column.shape[0]
    slots = column.shape[-1]
    core = lax.axis_index("gy")
    for at in range(2 * cells):
        cell = beside[at] if at < cells else column[at - cells]
        coords = [cell[ROW_XYZ + i : ROW_XYZ + i + 1] for i in range(3)]
        vectors = [cell[NVEC * i : NVEC * i + NVEC] for i in range(3)]
        stacked = jnp.concatenate(source_moments(coords, vectors), axis=0)
        for part, value in enumerate(split3(stacked)):
            moments[at, part * COMPS * NVEC : (part + 1) * COMPS * NVEC, :] = value
        scale = lax.rsqrt(cell[ROW_POLAR : ROW_POLAR + 1])
        tail = jnp.concatenate(coords + [scale] + [jnp.zeros((4, slots), F32)], axis=0)
        sources[at] = tail.T
    fields[...] = jnp.zeros(fields.shape, F32)
    group_columns = jnp.concatenate([groups[...].astype(F32), jnp.zeros((6, slots), F32)], 0).T

    def one_block(index, inside_check):
        source, target, own_at, inside, move_x, move_y = block_of(index, core, cells)
        rows = column[target, ROW_XYZ : ROWS, :]
        place = moved_target(rows, move_x, move_y)
        scale = lax.rsqrt(rows[3:4]) * (-THOLE_DAMP / LN2)
        if inside_check:
            group = groups[pl.ds(own_at, 1), :].astype(F32)
            group = jnp.where(inside, group, -1.0)
        for chunk in range(slots // CHUNK):
            part = pl.ds(chunk * CHUNK, CHUNK)
            near = sources[source, part, :]
            dx = near[:, 0:1] - place[0]
            dy = near[:, 1:2] - place[1]
            dz = near[:, 2:3] - place[2]
            square = (dx * dx + dy * dy) + dz * dz + SOFTENING
            inverse = lax.rsqrt(square)
            inverse_sq = inverse * inverse
            inverse_cube = inverse_sq * inverse
            exponent = (square * square * inverse) * (near[:, 3:4] * scale)
            damping = jnp.exp2(exponent)
            taper = jnp.maximum(1.0 - square * (1.0 / CUTOFF_SQ), 0.0)
            weight = taper * taper * inverse_cube
            if inside_check:
                keys = jnp.where(own_at == 0, group_part0[chunk], group_part1[chunk])
                weight = jnp.where(keys == group, 0.0, weight)
            isotropic = weight * (1.0 - damping)
            tensorial = weight * inverse_sq * (1.0 - (1.0 - LN2 * exponent) * damping)
            for at, value in enumerate(split3(tensorial) + split2(isotropic)):
                pairs[index, at, part, :] = value
        lhs = moments[source]
        size = COMPS * NVEC
        first = jnp.dot(lhs, pairs[index, 0], preferred_element_type=F32)
        second = jnp.dot(lhs[: 2 * size], pairs[index, 1], preferred_element_type=F32)
        third = jnp.dot(lhs[:size], pairs[index, 2], preferred_element_type=F32)
        total = (first[:size] + first[size : 2 * size] + first[2 * size :]) + (
            second[:size] + second[size:] + third
        )
        low = size - 4 * NVEC
        iso_lhs = jnp.concatenate([lhs[low:size], lhs[size + low : 2 * size], lhs[2 * size + low :]], 0)
        first = jnp.dot(iso_lhs, pairs[index, 3], preferred_element_type=F32)
        second = jnp.dot(iso_lhs[: 8 * NVEC], pairs[index, 4], preferred_element_type=F32)
        band = 4 * NVEC
        iso = (first[:band] + first[band : 2 * band] + first[2 * band :]) + (
            second[:band] + second[band:]
        )
        result = fields_of(
            [total[NVEC * i : NVEC * i + NVEC] for i in range(COMPS)],
            [iso[NVEC * i : NVEC * i + NVEC] for i in range(1, 4)],
            place,
        )
        for i in range(3):
            fields[target, NVEC * i : NVEC * i + NVEC, :] += result[i]

    group_part0 = [group_columns[c * CHUNK : (c + 1) * CHUNK, 0:1] for c in range(slots // CHUNK)]
    group_part1 = [group_columns[c * CHUNK : (c + 1) * CHUNK, 1:2] for c in range(slots // CHUNK)]

    def near_body(index, carry):
        one_block(index, False)
        return carry

    def own_body(index, carry):
        one_block(index, True)
        return carry

    lax.fori_loop(0, 12, near_body, 0)
    lax.fori_loop(12, BLOCKS, own_body, 0)


def jacobi_kernel(shared, column, jacobi):
    for cell in range(column.shape[0]):
        scaled = column[cell, ROW_POLAR : ROW_POLAR + 1] * column[cell, ROW_OCC : ROW_OCC + 1]
        for i in range(3):
            row = NVEC * i + NVEC - 1
            field = shared[0, cell, row : row + 1] + shared[1, cell, row : row + 1]
            perm = column[cell, ROW_PERM + i : ROW_PERM + i + 1]
            jacobi[cell, i : i + 1, :] = scaled * (perm + field)


def apply_kernel(column, beside, jacobi, jacobi_beside, pairs, fields, moments):
    cells = column.shape[0]
    core = lax.axis_index("gy")
    for at in range(2 * cells):
        cell = beside[at] if at < cells else column[at - cells]
        vector = jacobi_beside[at] if at < cells else jacobi[at - cells]
        coords = [cell[ROW_XYZ + i : ROW_XYZ + i + 1] for i in range(3)]
        vectors = [vector[i : i + 1] for i in range(3)]
        stacked = jnp.concatenate(source_moments(coords, vectors), axis=0)
        for part, value in enumerate(split3(stacked)):
            moments[at, part * COMPS : (part + 1) * COMPS, :] = value
    fields[...] = jnp.zeros(fields.shape, F32)

    def one_block(index, carry):
        source, target, own_at, inside, move_x, move_y = block_of(index, core, cells)
        place = moved_target(column[target, ROW_XYZ : ROWS, :], move_x, move_y)
        lhs = moments[source]
        first = jnp.dot(lhs, pairs[index, 0], preferred_element_type=F32)
        second = jnp.dot(lhs[: 2 * COMPS], pairs[index, 1], preferred_element_type=F32)
        third = jnp.dot(lhs[:COMPS], pairs[index, 2], preferred_element_type=F32)
        total = (first[:COMPS] + first[COMPS : 2 * COMPS] + first[2 * COMPS :]) + (
            second[:COMPS] + second[COMPS:] + third
        )
        first = jnp.dot(lhs, pairs[index, 3], preferred_element_type=F32)
        second = jnp.dot(lhs[: 2 * COMPS], pairs[index, 4], preferred_element_type=F32)
        iso = (first[:COMPS] + first[COMPS : 2 * COMPS] + first[2 * COMPS :]) + (
            second[:COMPS] + second[COMPS:]
        )
        result = fields_of(
            [total[i : i + 1] for i in range(COMPS)],
            [iso[i : i + 1] for i in range(COMPS - 3, COMPS)],
            place,
        )
        for i in range(3):
            fields[target, i : i + 1, :] += result[i]
        return carry

    lax.fori_loop(0, BLOCKS, one_block, 0)


def own_vectors(core, cell, i, column, jacobi, shared, shared_last):
    at = 2 * core + cell
    slots = column.shape[-1]
    last = lax.broadcasted_iota(jnp.int32, (NVEC, slots), 0) == NVEC - 1
    rows = slice(NVEC * i, NVEC * i + NVEC)
    vectors = column[at, rows, :]
    current = vectors[NVEC - 1 :]
    jacobi_row = jacobi[at, i : i + 1, :]
    vectors = jnp.where(last, jacobi_row, vectors)
    field = shared[0, at, rows, :] + shared[1, at, rows, :]
    newest = shared_last[0, at, i : i + 1, :] + shared_last[1, at, i : i + 1, :]
    field = jnp.where(last, newest, field)
    scaled = column[at, ROW_POLAR : ROW_POLAR + 1, :] * column[at, ROW_OCC : ROW_OCC + 1, :]
    perm = column[at, ROW_PERM + i : ROW_PERM + i + 1, :]
    return vectors, field, current, jacobi_row, scaled, perm


def gram_kernel(column, jacobi, shared, shared_last, past_res, gram):
    core = lax.axis_index("gy")
    slots = column.shape[-1]
    last = lax.broadcasted_iota(jnp.int32, (NVEC, slots), 0) == NVEC - 1
    total = jnp.zeros((2 * NVEC, 4 * NVEC * NVEC), F32)
    for cell in range(past_res.shape[0]):
        occ = column[2 * core + cell, ROW_OCC : ROW_OCC + 1, :]
        for i in range(3):
            vectors, field, current, newest, scaled, perm = own_vectors(
                core, cell, i, column, jacobi, shared, shared_last
            )
            old = [past_res[cell, k, i : i + 1, :] for k in range(NVEC - 1)]
            residual = jnp.concatenate(old + [newest - current], axis=0) * occ
            implied = scaled * (perm + field) - vectors
            both = jnp.concatenate([residual, implied], axis=0)
            many = jnp.concatenate([both] * (2 * NVEC), axis=0)
            total = total + lax.dot_general(
                both,
                many,
                (((1,), (1,)), ((), ())),
                precision=lax.Precision.HIGHEST,
                preferred_element_type=F32,
            )
    shape = total.shape
    row = lax.broadcasted_iota(jnp.int32, shape, 0)
    lane = lax.broadcasted_iota(jnp.int32, shape, 1)
    flat = jnp.sum(jnp.where(lane // (2 * NVEC) == row, total, 0.0), axis=0, keepdims=True)
    half = shape[1] // 2
    gram[0:1, :] = flat[:, :half]
    gram[1:2, :] = flat[:, half:]


def solve_ones(matrix):
    size = len(matrix)
    lower = [[None] * size for _ in range(size)]
    inverse = [None] * size
    scaled = [[None] * size for _ in range(size)]
    for j in range(size):
        for i in range(j, size):
            value = matrix[i][j]
            for k in range(j):
                value = value - scaled[i][k] * lower[j][k]
            scaled[i][j] = value
        inverse[j] = 1.0 / scaled[j][j]
        for i in range(j + 1, size):
            lower[i][j] = scaled[i][j] * inverse[j]
    forward = []
    for i in range(size):
        value = jnp.ones_like(inverse[0])
        for k in range(i):
            value = value - lower[i][k] * forward[k]
        forward.append(value)
    backward = [None] * size
    for i in reversed(range(size)):
        value = forward[i] * inverse[i]
        for k in range(i + 1, size):
            value = value - lower[k][i] * backward[k]
        backward[i] = value
    total = sum(backward[1:], backward[0])
    return [value / total for value in backward]


def finish_kernel(partials, column, jacobi, shared, shared_last, dipoles, weights):
    core = lax.axis_index("gy")
    slots = column.shape[-1]
    lanes = partials.shape[-1]
    summed = partials[0]
    for k in range(1, partials.shape[0]):
        summed = summed + partials[k]

    def entry(k, j):
        flat = k * 2 * NVEC + j
        row, lane = flat // lanes, flat % lanes
        return jnp.broadcast_to(summed[row : row + 1, lane : lane + 1], (1, lanes))

    first = [[entry(j, k) if j <= k else None for j in range(NVEC)] for k in range(NVEC)]
    early = solve_ones(first)
    mixed = []
    for k in range(1, NVEC):
        value = early[0] * entry(k, NVEC)
        for m in range(1, NVEC):
            value = value + early[m] * entry(k, NVEC + m)
        mixed.append(value)
    square = None
    for m in range(NVEC):
        value = 0.5 * early[m] * entry(NVEC + m, NVEC + m)
        for n in range(m + 1, NVEC):
            value = value + early[n] * entry(NVEC + m, NVEC + n)
        value = early[m] * value
        square = value if square is None else square + value
    second = [
        [first[k][j] if j <= k else None for j in range(1, NVEC)] + [None]
        for k in range(1, NVEC)
    ]
    second.append(mixed + [2.0 * square])
    late = solve_ones(second)

    sub = lax.broadcasted_iota(jnp.int32, (NVEC, lanes), 0)
    lane = lax.broadcasted_iota(jnp.int32, (1, lanes), 1)
    early_column = jnp.zeros((NVEC, lanes), F32)
    late_column = jnp.zeros((NVEC, lanes), F32)
    row = jnp.zeros((1, lanes), F32)
    for k in range(NVEC):
        early_column = jnp.where(sub == k, early[k], early_column)
        if k:
            late_column = jnp.where(sub == k, late[k - 1], late_column)
        row = jnp.where(lane == k, late[k], row)
    weights[...] = row
    reach = slots // lanes
    early_column = jnp.concatenate([early_column] * reach, axis=1)
    late_column = jnp.concatenate([late_column] * reach, axis=1)
    last = jnp.concatenate([late[NVEC - 1]] * reach, axis=1)
    for cell in range(dipoles.shape[0]):
        for i in range(3):
            vectors, field, current, newest, scaled, perm = own_vectors(
                core, cell, i, column, jacobi, shared, shared_last
            )
            induced = jnp.sum(early_column * field, axis=0, keepdims=True)
            output = scaled * (perm + induced)
            kept = jnp.sum(late_column * vectors, axis=0, keepdims=True)
            dipoles[cell, i : i + 1, :] = kept + last * output


def call(kernel, out_shape, operands, specs=None, scratch=(), megabytes=16):
    single = not isinstance(out_shape, (list, tuple))
    outs = [out_shape] if single else list(out_shape)
    result = pl.pallas_call(
        kernel,
        out_shape=outs,
        in_specs=specs or [vmem() for _ in operands],
        out_specs=[vmem() for _ in outs],
        scratch_shapes=list(scratch),
        compiler_params=pltpu.CompilerParams(vmem_limit_bytes=megabytes << 20),
    )(*operands)
    return result[0] if single else result


def shape_of(*dims, dtype=F32):
    return jax.ShapeDtypeStruct(dims, dtype)


def sideways(block):
    count = lax.axis_size(GX)
    cores = lax.axis_size("gy")
    route = []
    for x in range(count):
        for core in range(cores):
            source = (x + 1 - 2 * core) % count
            route.append((source * cores + core, x * cores + core))
    return lax.ppermute(block, GX + ("gy",), route)


def exchanged(block, axes):
    size = lax.axis_size(axes)
    many = jnp.broadcast_to(block[None], (size,) + block.shape)
    return lax.all_to_all(many, axes, 0, 0)


def body(
    positions, polarizability, tile_counts, molecules, perm_field, dipoles, past_out, past_res
):
    own_cells, slots = positions.shape[1], positions.shape[-1]
    packed = call(
        pack_kernel,
        shape_of(own_cells, ROWS, slots),
        (tile_counts[0], positions[0], polarizability[0], perm_field[0], dipoles[0], past_out[0]),
        [smem()] + [vmem()] * 5,
    )
    column = lax.all_gather(packed, "gy").reshape(-1, ROWS, slots)
    cells = column.shape[0]
    beside = sideways(column)
    partial, pairs = call(
        pair_kernel,
        [shape_of(cells, 3 * NVEC, slots), shape_of(BLOCKS, 5, slots, slots, dtype=BF16)],
        (column, beside, molecules[0]),
        scratch=[
            pltpu.VMEM((2 * cells, 3 * COMPS * NVEC, slots), BF16),
            pltpu.VMEM((2 * cells, slots, 8), F32),
        ],
        megabytes=48,
    )
    shared = lax.all_gather(partial, "gy")
    jacobi = call(jacobi_kernel, shape_of(cells, 3, slots), (shared, column))
    jacobi_beside = sideways(jacobi)
    partial_last = call(
        apply_kernel,
        shape_of(cells, 3, slots),
        (column, beside, jacobi, jacobi_beside, pairs),
        scratch=[pltpu.VMEM((2 * cells, 3 * COMPS, slots), BF16)],
        megabytes=40,
    )
    shared_last = lax.all_gather(partial_last, "gy")
    gram = call(
        gram_kernel,
        shape_of(2, 2 * NVEC * NVEC),
        (column, jacobi, shared, shared_last, past_res[0]),
    )
    gram = jnp.sum(exchanged(gram, ("gx_1", "gy")), axis=0)
    partials = exchanged(gram, ("gx_0",))
    following, weights = call(
        finish_kernel,
        [shape_of(own_cells, 3, slots), shape_of(1, 2 * NVEC * NVEC)],
        (partials, column, jacobi, shared, shared_last),
    )
    return (following[None], weights[0, :NVEC])


def solution(mesh):
    torus = Mesh(
        mesh.devices.reshape(mesh.shape["box"], TORUS_Z, TORUS_X, mesh.shape["gy"]),
        ("box", "gx_0", "gx_1", "gy"),
    )
    return jax.shard_map(
        body,
        mesh=torus,
        in_specs=(
            P(BOX_GX, "gy", None, None),
            P(BOX_GX, "gy", None),
            P(BOX_GX, "gy", None),
            P(BOX_GX, "gy", None),
            P(BOX_GX, "gy", None, None),
            P(BOX_GX, "gy", None, None),
            P(BOX_GX, "gy", None, None, None),
            P(BOX_GX, "gy", None, None, None),
        ),
        out_specs=(P(BOX_GX, "gy", None, None), P("box")),
        check_vma=False,
    )
```

time: 359 us -> 130 us (0.36)
  between operations: 93.1 us -> 0.7 us
  blocking collectives: 89.9 us -> 34.5 us
  other arithmetic: 47 us -> 0.03 us
  starting transfers between devices: 92.8 us -> 55 us
  Pallas kernels: 0 us -> 25.2 us
  waiting for transfers between devices: 15.6 us -> 3.11 us
  local copies, waits for them, and re-layouts: 15.3 us -> 10.5 us
    psum x6 -> x0, blocking collectives: 89.9 us -> none  [one_axis_at_a_time(): return functools.reduce(lax.psum, axes, array)]
    ppermute x20 -> x2, starting transfers between devices: 92.8 us -> 55 us  [sideways(): return lax.ppermute(block, GX + ('gy',), route)]
    all_to_all x0 -> x2, blocking collectives: none -> 28.7 us  [exchanged(): return lax.all_to_all(many, axes, 0, 0)]
    pallas_call x0 -> x6, Pallas kernels: none -> 25.2 us  [call(): pl.pallas_call(kernel, out_shape=outs, in_specs=specs or [vmem() for _ in...]
    reduce_sum x50 -> x1, other arithmetic: 20 us -> 0.03 us  [body(): gram = jnp.sum(exchanged(gram, ('gx_1', 'gy')), axis=0)]
    ppermute x20 -> x2, waiting for transfers between devices: 15.6 us -> 3.11 us  [sideways(): return lax.ppermute(block, GX + ('gy',), route)]
    div x20 -> x0, other arithmetic: 10.8 us -> none  [the longest x16 10.8 us: pair_terms(): isotropic = weight * -jnp.expm1(-damped) / cube_dist]
    mul x20 -> x0, other arithmetic: 9.21 us -> none  [the longest x8 7.77 us: field_targets(): tensorial * projected]
  transfers between devices with their start and end apart: 20 -> 2, of which waited for: 5 -> 2; matrix products, arithmetic and copies ran while one was open for 2% -> 1% of each run, Pallas kernels for 0% -> 0%
where the time goes in v1:
time: 130 us; the launch traced here: 129 us
  starting transfers between devices  55 us (42%)
  blocking collectives  34.5 us (27%)
  Pallas kernels  25.2 us (19%)
  local copies, waits for them, and re-layouts  10.5 us (8%)
  waiting for transfers between devices  3.11 us (2%)
    ppermute x2, starting transfers between devices, sideways(): return lax.ppermute(block, GX + ('gy',), route)  55 us
    all_to_all x2, blocking collectives, exchanged(): return lax.all_to_all(many, axes, 0, 0)  28.7 us
    pallas_call x6, Pallas kernels, call(): pl.pallas_call(kernel, out_shape=outs, in_specs=specs or [vmem() for _ in...  25.2 us
    unnamed x12, local copies, waits for them, and re-layouts  9.29 us
    ppermute x2, waiting for transfers between devices, sideways(): return lax.ppermute(block, GX + ('gy',), route)  3.11 us
  transfers between devices with their start and end apart: 2, of which 2 were waited for; matrix products, arithmetic and copies ran while one was open for 1% of the time, Pallas kernels for 0%

profile of v1, /device:TPU:80, one launch (start us, length us, event | category | flops | bytes accessed | tf_op | source)
XLA Modules:
  0.0 129.1 jit_solution(938590797101539777)
XLA Ops:
  0.6 0.8 copy.42
  1.4 0.7 copy.43
  2.1 0.7 copy_bitcast_fusion.2
  2.8 0.0 copy-start.1
  2.8 0.7 copy-done.1
  3.5 0.0 copy-start.3
  3.5 0.7 copy-done.3
  4.2 0.6 shard_map.95
  4.8 2.0 %all-gather.column = f32[4,32,256]{2,1,0:T(8,128)S(1)} all-gather(f32[2,32,256]{2,1,0:T(8,128)S(1)} %shard_map.95), channel_id=2, replica_groups=mesh['box'=2,'gx_0'=16,'gx_1'=8,'gy'=2] {'gy'}, dimensions={0}, use_global_device_ids=true | all-gather | bytes 196608 | tf_op jit(solution)/shard_map/all_gather | solution.py:441
  6.8 47.3 %collective-permute-start = (f32[4,32,256]{2,1,0:T(8,128)S(1)}, f32[4,32,256]{2,1,0:T(8,128)S(1)}, u32[]{:S(2)}, u32[]{:S(2)}) collective-permute-start(f32[4,32,256]{2,1,0:T(8,128)S(1)} %all-gather.column), channel_id=1, source_target_pairs={{2,0},{255,1},{4,2},{1,3},{6,4},{3,5},{8,6},{5,7},{10,8},{7,9},{12... | collective-permute-start | bytes 393224 | tf_op jit(solution)/shard_map/ppermute | solution.py:422
  54.0 2.5 %collective-permute-done.beside = f32[4,32,256]{2,1,0:T(8,128)S(1)} collective-permute-done((f32[4,32,256]{2,1,0:T(8,128)S(1)}, f32[4,32,256]{2,1,0:T(8,128)S(1)}, u32[]{:S(2)}, u32[]{:S(2)}) %collective-permute-start) | collective-permute-done | bytes 131104 | tf_op jit(solution)/shard_map/ppermute | solution.py:422
  56.5 0.0 copy-start.2
  56.5 0.7 copy-done.2
  57.2 18.3 %shard_map.96 = (f32[4,24,256]{2,1,0:T(8,128)S(1)}, bf16[18,5,256,256]{3,2,1,0:T(8,128)(2,1)}) custom-call(f32[4,32,256]{2,1,0:T(8,128)S(1)} %all-gather.column, f32[4,32,256]{2,1,0:T(8,128)S(1)} %collective-permute-done.beside, s32[2,256]{1,0:T(2,128)S(1)} %bitcast.31), custom_call_target="tpu_custom_call" | custom-call | tf_op jit(solution)/shard_map/pallas_call | solution.py:399
  75.5 2.0 %all-gather.1 = f32[8,24,256]{2,1,0:T(8,128)S(1)} all-gather(f32[4,24,256]{2,1,0:T(8,128)S(1)} %get-tuple-element.6), channel_id=3, replica_groups=mesh['box'=2,'gx_0'=16,'gx_1'=8,'gy'=2] {'gy'}, dimensions={0}, use_global_device_ids=true | all-gather | bytes 294912 | tf_op jit(solution)/shard_map/all_gather | solution.py:454
  77.5 7.7 %collective-permute-start.1 = (f32[4,3,256]{2,1,0:T(4,128)S(1)}, f32[4,3,256]{2,1,0:T(4,128)S(1)}, u32[]{:S(2)}, u32[]{:S(2)}) collective-permute-start(f32[4,3,256]{2,1,0:T(4,128)S(1)} %shard_map.97.jacobi), channel_id=1, source_target_pairs={{2,0},{255,1},{4,2},{1,3},{6,4},{3,5},{8,6},{5,7},{10,8},{7,9},{12... | collective-permute-start | bytes 36872 | tf_op jit(solution)/shard_map/ppermute | solution.py:422
  85.2 0.8 copy.41
  86.0 0.6 collective-permute-done.1.jacobi_beside
  86.6 0.0 copy-start
  86.6 4.3 %copy-done = bf16[18,5,256,256]{3,2,1,0:T(8,128)(2,1)S(1)} copy-done((bf16[18,5,256,256]{3,2,1,0:T(8,128)(2,1)S(1)}, bf16[18,5,256,256]{3,2,1,0:T(8,128)(2,1)}, u32[]{:S(2)}) %copy-start) | copy-done | bytes 11796504
  90.9 4.7 %shard_map.98 = f32[4,3,256]{2,1,0:T(4,128)S(1)} custom-call(f32[4,32,256]{2,1,0:T(8,128)S(1)} %all-gather.column, f32[4,32,256]{2,1,0:T(8,128)S(1)} %collective-permute-done.beside, f32[4,3,256]{2,1,0:T(4,128)S(1)} %shard_map.97.jacobi, f32[4,3,256]{2,1,0:T(4,128)S(1)} %collective-permute-done.1.jacobi_beside, bf16[18,5,256,256]{3,2,1,0:T(8,128)(2,1)S(1)} %copy-done), custom_call_target="tpu_custom_call" | custom-call | tf_op jit(solution)/shard_map/pallas_call | solution.py:399
  95.6 1.9 %all-gather.2 = f32[8,3,256]{2,1,0:T(4,128)S(1)} all-gather(f32[4,3,256]{2,1,0:T(4,128)S(1)} %shard_map.98), channel_id=4, replica_groups=mesh['box'=2,'gx_0'=16,'gx_1'=8,'gy'=2] {'gy'}, dimensions={0}, use_global_device_ids=true | all-gather | bytes 36864 | tf_op jit(solution)/shard_map/all_gather | solution.py:464
  97.5 1.4 %shard_map.99 = f32[2,128]{1,0:T(2,128)S(1)} custom-call(f32[4,32,256]{2,1,0:T(8,128)S(1)} %all-gather.column, f32[4,3,256]{2,1,0:T(4,128)S(1)} %shard_map.97.jacobi, f32[2,4,24,256]{3,2,1,0:T(8,128)S(1)} %bitcast.22, f32[2,4,3,256]{3,2,1,0:T(4,128)S(1)} %bitcast.24, f32[2,7,3,256]{3,2,1,0:T(4,128)S(1)} %bitcast.27), custom_call_target="tpu_custom_call" | custom-call | tf_op jit(solution)/shard_map/pallas_call | solution.py:399
  98.9 10.3 %all_to_all.10 = f32[16,2,128]{2,1,0:T(2,128)S(1)} all-to-all(f32[16,2,128]{2,1,0:T(2,128)S(1)} %broadcast_in_dim.6), channel_id=1, replica_groups=mesh['box'=2,'gx_0'=16,'gx_1'=8,'gy'=2] {'gx_1','gy'}, dimensions={0} | all-to-all | bytes 32768 | tf_op jit(solution)/shard_map/all_to_all | solution.py:428
  109.2 18.4 %all_to_all.11.partials = f32[16,2,128]{2,1,0:T(2,128)S(1)} all-to-all(f32[16,2,128]{2,1,0:T(2,128)S(1)} %broadcast_in_dim.7), channel_id=1, replica_groups=mesh['box'=2,'gx_0'=16,'gx_1'=8,'gy'=2] {'gx_0'}, dimensions={0} | all-to-all | bytes 32768 | tf_op jit(solution)/shard_map/all_to_all | solution.py:428
  127.6 0.4 shard_map.100
  128.0 0.6 copy.34
  128.6 0.5 slice_bitcast_fusion
  (4 shorter events, 0.1 us)
Async XLA Ops:
  2.8 0.7 copy-start.1
  3.5 0.7 copy-start.3
  6.8 49.8 %collective-permute-start = (f32[4,32,256]{2,1,0:T(8,128)S(1)}, f32[4,32,256]{2,1,0:T(8,128)S(1)}, u32[]{:S(2)}, u32[]{:S(2)}) collective-permute-start(f32[4,32,256]{2,1,0:T(8,128)S(1)} %all-gather.column), channel_id=1, source_target_pairs={{2,0},{255,1},{4,2},{1,3},{6,4},{3,5},{8,6},{5,7},{10,8},{7,9},{12... | collective-permute-start | bytes 393224 | tf_op jit(solution)/shard_map/ppermute | solution.py:422
  56.5 0.7 copy-start.2
  77.5 9.1 %collective-permute-start.1 = (f32[4,3,256]{2,1,0:T(4,128)S(1)}, f32[4,3,256]{2,1,0:T(4,128)S(1)}, u32[]{:S(2)}, u32[]{:S(2)}) collective-permute-start(f32[4,3,256]{2,1,0:T(4,128)S(1)} %shard_map.97.jacobi), channel_id=1, source_target_pairs={{2,0},{255,1},{4,2},{1,3},{6,4},{3,5},{8,6},{5,7},{10,8},{7,9},{12... | collective-permute-start | bytes 36872 | tf_op jit(solution)/shard_map/ppermute | solution.py:422
  86.6 4.4 %copy-start = (bf16[18,5,256,256]{3,2,1,0:T(8,128)(2,1)S(1)}, bf16[18,5,256,256]{3,2,1,0:T(8,128)(2,1)}, u32[]{:S(2)}) copy-start(bf16[18,5,256,256]{3,2,1,0:T(8,128)(2,1)} %get-tuple-element.7.pairs) | copy-start | bytes 35389444
